TPU v7x, 256 devices: a whole 4x4x8 slice. The times are simulated.
256 devices in a mesh: dp: 32 (over y, z), group: 8 (over x, core).
Axes of the slice: x: 4, y: 4, z: 8, core: 2. Of those that a mesh axis runs over, the one named last changes fastest.
Arguments:
- keys: int32 [131072], P(('dp', 'group')), may hold values from 0 to 1073741823
- cut: int32 [1], replicated, may hold values from 256 to 1023
- owner: int32 [131072, 1], P(('dp', 'group')), may hold values from 0 to 31; in each aligned block of 512 rows (0 to 511, 512 to 1023, ...) at most 32 rows name the same one
- tokens: int32 [131072, 2048], P(('dp', 'group')), may hold values from 0 to 128255
Outputs:
- histogram: int32 [4096], replicated
- packed_rows: int32 [262144, 2048], P(('dp', 'group'))
- packed_weights: float32 [262144], P(('dp', 'group'))
Inputs may be any that keep to these rules, and one draw needn't show every extreme that they name: Among the examples of one device, at most 32 have the same owner, and some owner has exactly 32.
All inputs are finite; a program needn't handle non-finite values.
Results may differ from a plain program's by a relative error of at most 0.0003.
Values sent between devices are 32-bit elements; how exact they have to be, the bound alone decides.
A program may use at most 128 MiB of HBM per device.

v0:
```python
import functools

import jax
import jax.numpy as jnp
from jax import lax
from jax.experimental import pallas as pl
from jax.experimental.pallas import tpu as pltpu
from jax.sharding import Mesh
from jax.sharding import PartitionSpec as P

BINS = 4096
BIN_WIDTH = 262144
NY, NZ, NX, NC = 4, 8, 4, 2
NO = NY * NZ
NM = NX * NC
NS = NO * NM
PLANE = NY * NM
EX = 512
RECV = 1024
MESH_ID = pl.DeviceIdType.MESH
AXES = ("y", "z", "x", "c")

TIERS = (
    (204, 164, 118, 70),
    (222, 180, 132, 84),
    (254, 202, 154, 94),
    (384, 264, 256, 128),
)
PLUS, OWN, MINUS = 0, 384, 512
PACKED = 896


def me():
    return tuple(lax.axis_index(a) for a in AXES)


def signal_all(bar, z, y, x, c):
    def ring(d, _):
        pl.semaphore_signal(bar, 1, device_id={"z": lax.rem(z + d, NZ)}, device_id_type=MESH_ID)
        return 0

    def plane(r, _):
        pl.semaphore_signal(bar, 1, device_id=in_plane(r, y, x, c), device_id_type=MESH_ID)
        return 0

    lax.fori_loop(1, NZ, ring, 0)
    lax.fori_loop(1, PLANE, plane, 0)


def plane_of(r, y, x, c):
    to = in_plane(r, y, x, c)
    return to["y"] * NM + to["x"] * NC + to["c"]


def in_plane(r, y, x, c):
    return {
        "y": lax.rem(y + lax.div(r, NM), NY),
        "x": lax.rem(x + lax.rem(lax.div(r, NC), NX), NX),
        "c": lax.rem(c + lax.rem(r, NC), NC),
    }

HIGHEST = lax.Precision.HIGHEST
F32, BF16, I32 = jnp.float32, jnp.bfloat16, jnp.int32


def batched(lo, hi, load, store, batch=16):
    def step(b, count):
        for k, value in enumerate([load(b, k) for k in range(count)]):
            store(b, k, value)

    def run(b, _):
        step(lo + b * batch, batch)
        return 0

    full = (hi - lo) // batch
    lax.fori_loop(0, full, run, 0)
    step(lo + full * batch, (hi - lo) % batch)


def put(ref):
    def store(b, k, value):
        ref[b + k] = value

    return store


def iota(shape, dim):
    return lax.broadcasted_iota(I32, shape, dim)


def mul(a, b, contract=(1, 0), exact=False):
    dims = (((contract[0],), (contract[1],)), ((), ()))
    if exact:
        return lax.dot_general(a.astype(F32), b.astype(F32), dims, precision=HIGHEST, preferred_element_type=F32)
    return lax.dot_general(a.astype(BF16), b.astype(BF16), dims, preferred_element_type=F32)


def tmul(a, b, exact=False):
    return mul(a, b, (0, 0), exact)


def f32(mask):
    return jnp.where(mask, 1.0, 0.0).astype(F32)


def source_of(t):
    p, z = t >> 3, t & 7
    return ((p >> 3) * NZ + z) * NM + (p & 7)


L_FIRST, L_SPLIT, L_HOP, L_BIN = 32, 64, 65, 96


def stats_kernel(cut_ref, keys_hbm, owner_hbm, tok_hbm,
                 table_ref, idx_ref, src_ref, tier_ref, bins_ref, hist_ref, rows_ref,
                 tok_ref, keys_ref, owner_ref, row_ref, ring_ref,
                 tok_sem, keys_sem, owner_sem, send1, send2, recv1, recv2):
    y, z, x, c = me()
    load_keys = pltpu.make_async_copy(keys_hbm, keys_ref, keys_sem)
    load_owner = pltpu.make_async_copy(owner_hbm, owner_ref, owner_sem)
    load = pltpu.make_async_copy(tok_hbm, tok_ref, tok_sem)
    load_keys.start()
    load_owner.start()
    load.start()
    bar = pltpu.get_barrier_semaphore()
    signal_all(bar, z, y, x, c)
    load_keys.wait()
    load_owner.wait()

    bins = lax.shift_right_logical(keys_ref[...], 18)
    dest = jnp.where(bins >= cut_ref[0], owner_ref[...], NO)
    hot = f32(iota((NO, EX), 0) == dest)
    before = mul(hot, f32(iota((EX, EX), 0) < iota((EX, EX), 1)))
    ones = jnp.ones((NO, 128), F32)
    count = mul(hot, jnp.ones((EX, 128), F32)).astype(I32)

    def place(o):
        delta = ((o & 7) - z) & 7
        side = jnp.where(delta == 4, 2, jnp.where(delta == 0, 3, jnp.where(delta < 4, 0, 1)))
        return delta, side, jnp.where(delta <= 4, 4 - delta, delta - 4) * NY + (o >> 3)

    d_row, s_row, p_row = place(iota((NO, NO), 0))
    d_col, s_col, p_col = place(iota((NO, NO), 1))
    inside = mul(f32((s_row == s_col) & (p_col < p_row)), count).astype(I32)
    bin_first = mul(f32((d_row == d_col) & (iota((NO, NO), 1) < iota((NO, NO), 0))), count).astype(I32)
    delta, side, _ = place(iota((NO, 128), 0))
    flow = lambda lo, hi: jnp.sum(jnp.where((delta >= lo) & (delta <= hi), count, 0), axis=0, keepdims=True)
    plus, minus, f4 = flow(1, 3), flow(5, 7), flow(4, 4)
    split = jnp.clip((f4 + minus - plus) >> 1, 0, f4)
    rest = f4 - split
    first = inside + jnp.where(side == 0, split, jnp.where(side == 1, rest, 0))
    hops = (
        jnp.maximum(plus + split, minus + rest),
        jnp.maximum(flow(2, 3) + split, flow(5, 6) + rest),
        jnp.maximum(flow(3, 3) + split, flow(5, 5) + rest),
        jnp.maximum(split, rest),
    )
    lane, o = iota((NO, 128), 1), iota((NO, 128), 0)
    row = jnp.where(lane == o, count, 0) + jnp.where(lane == L_FIRST + o, first, 0)
    row = row + jnp.where(lane == L_BIN + o, bin_first, 0)
    row = jnp.sum(row, axis=0, keepdims=True)
    lane = iota((1, 128), 1)
    row = row + jnp.where(lane == L_SPLIT, split, 0)
    for k, hop in enumerate(hops):
        row = row + jnp.where(lane == L_HOP + k, hop, 0)
    row = row.astype(F32)
    row_ref[0] = row
    ring_ref[pl.ds(z, 1)] = row.reshape(1, 1, 128)

    pl.semaphore_wait(bar, NZ - 1 + PLANE - 1)

    def start_ring(d, _):
        pltpu.make_async_remote_copy(
            row_ref.at[0], ring_ref.at[z], send1, recv1,
            device_id={"z": lax.rem(z + d, NZ)}, device_id_type=MESH_ID).start()
        return 0

    lax.fori_loop(1, NZ, start_ring, 0)

    rank = tmul(hot * before, ones).astype(I32)
    base = first + jnp.where(side == 1, MINUS, jnp.where(side == 3, OWN, 0))
    at = tmul(hot, base, exact=True).astype(I32) + rank
    far = tmul(hot, f32(side == 2)) > 0.5
    kept = tmul(hot, ones) > 0.5
    at = jnp.where(far & (at >= split), at + MINUS - split, at)
    at = jnp.where(kept, at, -1)
    e, lane = iota((EX, 128), 0), iota((EX, 128), 1)
    for g in range(PACKED // 128):
        src_ref[pl.ds(g, 1), :] = jnp.sum(jnp.where(at == g * 128 + lane, e, 0), axis=0, keepdims=True)

    pltpu.make_async_copy(ring_ref.at[pl.ds(0, NZ - 1)], ring_ref.at[pl.ds(0, NZ - 1)], recv1).wait()
    p = y * NM + x * NC + c

    def start_plane(r, _):
        pltpu.make_async_remote_copy(
            ring_ref, table_ref.at[p], send2, recv2,
            device_id=in_plane(r, y, x, c), device_id_type=MESH_ID).start()
        return 0

    lax.fori_loop(1, PLANE, start_plane, 0)
    table_ref[pl.ds(p, 1)] = ring_ref[...].reshape(1, NZ, 1, 128)

    bin_at = tmul(hot, (o & 7) * 128 + bin_first, exact=True).astype(I32) + rank
    bin_at = jnp.where(kept, bin_at, -1)
    part = iota((8, EX), 0)
    part = jnp.where(part == 0, bins >> 6, jnp.where(part == 1, bins & 63, 0))
    weight = jnp.where(iota((8, 128), 0) == 0, 64.0, 1.0)
    bin_col = tmul(part, weight)
    for k in range(NZ):
        bins_ref[k] = jnp.sum(jnp.where(bin_at == k * 128 + lane, bin_col, 0.0), axis=0, keepdims=True)
    hist = mul(f32(iota((32, EX), 0) == bins >> 7), f32(iota((128, EX), 0) == bins & 127), (1, 1))
    hist_ref[...] = hist.reshape(32, 1, 128)

    load.wait()

    def tiled(b, k):
        return tok_ref[pl.ds(b * 16 + (k // 8) * 128 + k % 8, 16, stride=8), :]

    batched(0, EX, tiled, put(rows_ref))

    others = table_ref.at[pl.ds(0, PLANE - 1)]
    pltpu.make_async_copy(others, others, recv2).wait()
    every = table_ref[...].reshape(NS, 128)

    top = jnp.max(every, axis=0, keepdims=True)
    lane = iota((1, 128), 1)
    tier = jnp.int32(0)
    for caps in TIERS[:-1]:
        cap = jnp.full((1, 128), 1e6, F32)
        for k in range(4):
            cap = jnp.where(lane == L_HOP + k, float(caps[k]), cap)
        over = jnp.where((lane >= L_HOP) & (lane < L_HOP + 4) & (top > cap), 1, 0)
        tier = tier + jnp.max(over)
    tier_ref[0] = tier

    zs, t = iota((NZ, NS), 0), iota((NZ, NS), 1)
    offset = mul(f32(source_of(t) < source_of(p * NZ + zs)), every).astype(I32) & 7
    lane, line = iota((128, 128), 1), iota((128, 128), 0)
    owner = ((y + (lane >> 5)) & 3) * NZ + z
    mine = ring_ref[...].reshape(NZ, 128)
    cnt = mul(mine, f32(line == owner)).astype(I32)
    off = mul(offset, f32(line == owner)).astype(I32)
    fst = mul(mine, f32(line == L_FIRST + owner), exact=True).astype(I32)
    spl = mul(mine, f32(line == L_SPLIT), exact=True).astype(I32)
    lane, zs = iota((NZ, 128), 1), iota((NZ, 128), 0)
    rel = lane >> 2
    member = ((x + (rel >> 1)) & 3) * NC + ((c + rel) & 1)
    lr = ((member - off) & 7) + NM * (lane & 3)
    q = fst + lr
    delta = (z - zs) & 7
    q = jnp.where((delta == 4) & (q >= spl), 128 + q - spl, q)
    q = jnp.where(delta == 0, OWN + q, q)
    idx_ref[...] = jnp.where(lr < cnt, q, 0)

    pltpu.make_async_copy(ring_ref.at[pl.ds(0, NZ - 1)], ring_ref.at[pl.ds(0, NZ - 1)], send1).wait()
    pltpu.make_async_copy(others, others, send2).wait()


def exchange_stats(cut, keys, owner, tokens):
    vmem, smem = pl.BlockSpec(memory_space=pltpu.VMEM), pl.BlockSpec(memory_space=pltpu.SMEM)
    hbm = pl.BlockSpec(memory_space=pltpu.HBM)
    dma = pltpu.SemaphoreType.DMA
    shape = jax.ShapeDtypeStruct
    return pl.pallas_call(
        stats_kernel,
        out_shape=(
            shape((PLANE, NZ, 1, 128), F32),
            shape((NZ, 128), I32),
            shape((PACKED // 128, 128), I32),
            shape((1,), I32),
            shape((NZ, 1, 128), F32),
            shape((32, 1, 128), F32),
            shape((EX, 16, 128), I32),
        ),
        in_specs=[smem, hbm, hbm, hbm],
        out_specs=(vmem, vmem, vmem, smem, vmem, vmem, vmem),
        scratch_shapes=[
            pltpu.VMEM((EX * 16, 128), I32),
            pltpu.VMEM((1, EX), I32),
            pltpu.VMEM((1, EX), I32),
            pltpu.VMEM((1, 1, 128), F32),
            pltpu.VMEM((NZ, 1, 128), F32),
            *[dma] * 7,
        ],
        compiler_params=pltpu.CompilerParams(
            collective_id=0, has_side_effects=True, vmem_limit_bytes=57 * 1024 * 1024),
        name="exchange_stats",
    )(cut, keys, owner, tokens)


def main_kernel(caps, cut_ref, idx_ref, src_ref, rows_ref, table_ref, bin_ref, hist_ref,
                rows_out, hist_out, weight_out, slot_out,
                pk, p1, m1, p2, m2, p3, m3, far, stage, hrs, hrow, hz, hrow2, hall, bz, ball,
                zsend, zrecv, psend, precv, hs1, hr1, hs2, hr2, hs3, hr3, bs1, br1, bs2, br2):
    y, z, x, c = me()
    bar = pltpu.get_barrier_semaphore()
    signal_all(bar, z, y, x, c)
    c1, c2, c3, c4 = caps
    up, down = lax.rem(z + 1, NZ), lax.rem(z + NZ - 1, NZ)
    plane = y * NM + x * NC + c

    def remote(src, dst, send, recv, to):
        copy = pltpu.make_async_remote_copy(src, dst, send, recv, device_id=to, device_id_type=MESH_ID)
        copy.start()
        return copy

    def loop(lo, hi, step):
        def run(i, _):
            step(i)
            return 0

        lax.fori_loop(lo, hi, run, 0)

    def whole(ref, n):
        return ref.at[pl.ds(0, n)]

    def wait(ref, n, sem):
        pltpu.make_async_copy(whole(ref, n), whole(ref, n), sem).wait()

    def hop(src, dst, lo, hi, at_src, at_dst, sem, to):
        return remote(src.at[pl.ds(at_src + lo, hi - lo)], dst.at[pl.ds(at_dst + lo, hi - lo)],
                      zsend.at[sem], zrecv.at[sem], {"z": to})

    def pack(lo, hi):
        batched(lo, hi, lambda b, k: rows_ref[src_ref[(b + k) >> 7, (b + k) & 127]], put(pk))

    pack(PLUS, PLUS + c1)
    pack(MINUS, MINUS + c1)
    pl.semaphore_wait(bar, NZ - 1 + PLANE - 1)

    loop(1, NZ, lambda d: remote(bin_ref.at[lax.rem(z + d, NZ)], bz.at[z], bs1, br1, {"z": lax.rem(z + d, NZ)}))
    h1 = [hop(pk, p1, 0, c2, PLUS, 0, 0, up), hop(pk, m1, 0, c2, MINUS, 0, 1, down),
          hop(pk, p1, c2, c1, PLUS, 0, 2, up), hop(pk, m1, c2, c1, MINUS, 0, 3, down)]
    bz[pl.ds(z, 1)] = bin_ref[pl.ds(z, 1)]
    pack(OWN, MINUS)

    def send_chunk(delta, src):
        zs = lax.rem(z + NZ - delta, NZ)
        base = delta * PLANE * 4

        batched(0, PLANE * 4, lambda b, k: src[idx_ref[zs, b + k]], lambda b, k, v: put(stage)(base + b, k, v))
        s = ((y * NZ + zs) * NX + x) * NC + c
        loop(1, PLANE, lambda r: remote(
            stage.at[pl.ds((delta * PLANE + r) * 4, 4)], rows_out.at[pl.ds(s * 4, 4)],
            psend, precv, in_plane(r, y, x, c)))
        pltpu.make_async_copy(
            stage.at[pl.ds(delta * PLANE * 4, 4)], rows_out.at[pl.ds(s * 4, 4)], precv).start()

    send_chunk(0, pk)

    loop(1, PLANE, lambda r: remote(hist_ref.at[plane_of(r, y, x, c)], hrs.at[plane], hs1, hr1, in_plane(r, y, x, c)))
    hrs[pl.ds(plane, 1)] = hist_ref[pl.ds(plane, 1)]
    wait(bz, NZ - 1, br1)
    ball[pl.ds(plane, 1)] = bz[...].reshape(1, NZ, 1, 128)
    loop(1, PLANE, lambda r: remote(bz, ball.at[plane], bs2, br2, in_plane(r, y, x, c)))
    wait(hrs, PLANE - 1, hr1)
    line = jnp.sum(hrs[...], axis=0, keepdims=True)
    hrow[...] = line
    hz[pl.ds(z, 1)] = line
    loop(1, NZ, lambda d: remote(hrow.at[0], hz.at[z], hs2, hr2, {"z": lax.rem(z + d, NZ)}))

    h1[0].wait_recv()
    h2 = [hop(p1, p2, 0, c3, 0, 0, 4, up)]
    h1[1].wait_recv()
    h2 += [hop(m1, m2, 0, c3, 0, 0, 5, down), hop(p1, p2, c3, c2, 0, 0, 6, up), hop(m1, m2, c3, c2, 0, 0, 7, down)]
    h1[2].wait_recv()
    send_chunk(1, p1)
    h1[3].wait_recv()
    send_chunk(7, m1)

    wait(hz, NZ - 1, hr2)
    line = jnp.sum(hz[...], axis=0, keepdims=True)
    hrow2[...] = line
    hall[pl.ds(plane, 1)] = line
    loop(1, PLANE, lambda r: remote(hrow2.at[0], hall.at[plane], hs3, hr3, in_plane(r, y, x, c)))

    every = table_ref[...].reshape(NS, 128)
    mine, member = y * NZ + z, x * NC + c
    line, lane = iota((128, 128), 0), iota((128, 128), 1)
    lower = f32(source_of(iota((NS, NS), 1)) < source_of(iota((NS, NS), 0)))
    cnt = mul(every, f32(line == mine)).astype(I32)
    off = mul(lower, every).astype(I32) & 7
    off = mul(off, f32(line == mine)).astype(I32)
    bin_first = mul(every, f32(line == L_BIN + mine)).astype(I32)
    lr0 = (member - off) & 7
    n = jnp.where(cnt > lr0, (cnt - lr0 + 7) >> 3, 0)
    start = mul(lower, n).astype(I32)
    s_row, t_lane = source_of(iota((NS, 128), 0)), iota((NS, 128), 1)
    for g in range(RECV // 128):
        j = g * 128 + t_lane - start
        slot = jnp.sum(jnp.where((j >= 0) & (j < n), 4 * s_row + j + 1, 0), axis=0, keepdims=True) - 1
        slot_out[pl.ds(g, 1), :] = slot

    h2[0].wait_recv()
    h3 = [hop(p2, p3, 0, c4, 0, 0, 8, up)]
    h2[1].wait_recv()
    h3 += [hop(m2, m3, 0, c4, 0, 0, 9, down), hop(p2, p3, c4, c3, 0, 0, 10, up), hop(m2, m3, c4, c3, 0, 0, 11, down)]
    h2[2].wait_recv()
    send_chunk(2, p2)
    h2[3].wait_recv()
    send_chunk(6, m2)
    h3[0].wait_recv()
    h4 = [hop(p3, far, 0, c4, 0, 0, 12, up)]
    h3[1].wait_recv()
    h4 += [hop(m3, far, 0, c4, 0, 128, 13, down)]
    h3[2].wait_recv()
    send_chunk(3, p3)
    h3[3].wait_recv()
    send_chunk(5, m3)
    h4[0].wait_recv()
    h4[1].wait_recv()
    send_chunk(4, far)

    wait(hall, PLANE - 1, hr3)
    wait(ball, PLANE - 1, br2)
    hist = hall[...].reshape(32, 128)
    hist_out[...] = hist.astype(I32)
    tail = mul(hist, f32(line >= lane), exact=True)
    above = jnp.sum(hist, axis=1, keepdims=True) + jnp.zeros((32, 128), F32)
    above = mul(f32(iota((32, 32), 1) > iota((32, 32), 0)), above, exact=True)
    suffix = tail + above
    bin_no = iota((32, 128), 0) * 128 + iota((32, 128), 1)
    total = jnp.maximum(jnp.sum(jnp.where(bin_no == cut_ref[0], suffix, 0.0)), 1.0)
    weights = suffix / total
    bins = ball[...].reshape(NS, 128).astype(I32)
    bins_hi, bins_lo = bins >> 7, bins & 127
    ones = jnp.ones((NS, 128), F32)
    for g in range(RECV // 128):
        j = g * 128 + t_lane - start
        hit = (j >= 0) & (j < n)
        hot = f32(hit)
        spot = tmul(jnp.where(hit, bin_first + lr0 + NM * j, 0), ones).astype(I32)
        some = tmul(hot, ones) > 0.5
        hi = jnp.sum(jnp.where(spot == lane, tmul(hot, bins_hi), 0.0), axis=1, keepdims=True).astype(I32)
        lo = jnp.sum(jnp.where(spot == lane, tmul(hot, bins_lo), 0.0), axis=1, keepdims=True).astype(I32)
        got = mul(f32(iota((128, 32), 1) == hi), weights, exact=True)
        got = jnp.sum(jnp.where((lane == lo) & some, got, 0.0), axis=1, keepdims=True)
        weight_out[pl.ds(g, 1), :] = jnp.sum(jnp.where(line == lane, got, 0.0), axis=0, keepdims=True)

    for copy in h1 + h2 + h3 + h4:
        copy.wait_send()
    wait(bz, NZ - 1, bs1)
    wait(ball, PLANE - 1, bs2)
    wait(hrs, PLANE - 1, hs1)
    wait(hz, NZ - 1, hs2)
    wait(hall, PLANE - 1, hs3)
    wait(stage, NZ * (PLANE - 1) * 4, psend)
    pltpu.make_async_copy(stage, rows_out, precv).wait()


def exchange_rows(tier, cut, idx, src, rows, table, bins, hist):
    caps = TIERS[tier]
    c1, c2, c3, c4 = caps
    vmem, smem = pl.BlockSpec(memory_space=pltpu.VMEM), pl.BlockSpec(memory_space=pltpu.SMEM)
    rows_of = lambda n: pltpu.VMEM((n, 16, 128), I32)
    lines = lambda *n: pltpu.VMEM((*n, 1, 128), F32)
    dma = pltpu.SemaphoreType.DMA
    shape = jax.ShapeDtypeStruct
    return pl.pallas_call(
        functools.partial(main_kernel, caps),
        out_shape=(
            shape((NS * 4, 16, 128), I32), shape((32, 128), I32),
            shape((RECV // 128, 128), F32), shape((RECV // 128, 128), I32),
        ),
        in_specs=[smem, smem, smem, vmem, vmem, vmem, vmem],
        out_specs=(pl.BlockSpec(memory_space=pl.ANY), vmem, vmem, vmem),
        scratch_shapes=[
            rows_of(PACKED), rows_of(c1), rows_of(c1), rows_of(c2), rows_of(c2), rows_of(c3), rows_of(c3),
            rows_of(256), rows_of(NS * 4),
            lines(PLANE), lines(1), lines(NZ), lines(1), lines(PLANE), lines(NZ), lines(PLANE, NZ),
            dma((14,)), dma((14,)), *[dma] * 12,
        ],
        compiler_params=pltpu.CompilerParams(
            collective_id=1 + tier, has_side_effects=True, vmem_limit_bytes=44 * 1024 * 1024),
        name=f"exchange_rows_{tier}",
    )(cut, idx, src, rows, table, bins, hist)


def unpack_kernel(slot_ref, rows_ref, hist_in, weight_in, out_ref, hist_out, weight_out):
    block = out_ref.shape[0] // 16
    first = pl.program_id(0) * block

    def load(b, k):
        row = slot_ref[first + b + k]
        return jnp.where(row >= 0, rows_ref[jnp.maximum(row, 0)], 0)

    def store(b, k, value):
        out_ref[pl.ds(b * 16 + (k // 8) * 128 + k % 8, 16, stride=8), :] = value

    batched(0, block, load, store)

    @pl.when(pl.program_id(0) == 0)
    def _():
        hist_out[...] = hist_in[...]
        weight_out[...] = weight_in[...]


def unpack_rows(slots, rows, hist, weights):
    block = 128
    vmem = pl.BlockSpec(memory_space=pltpu.VMEM)
    keep = lambda n: pl.BlockSpec((n, 128), lambda i: (0, 0))
    shape = jax.ShapeDtypeStruct
    return pl.pallas_call(
        unpack_kernel,
        grid=(RECV // block,),
        out_shape=(shape((RECV * 16, 128), I32), shape((32, 128), I32), shape((8, 128), F32)),
        in_specs=[pl.BlockSpec(memory_space=pltpu.SMEM), vmem, keep(32), keep(8)],
        out_specs=(pl.BlockSpec((block * 16, 128), lambda i: (i, 0)), keep(32), keep(8)),
        compiler_params=pltpu.CompilerParams(vmem_limit_bytes=24 * 1024 * 1024),
        name="unpack_rows",
    )(slots, rows, hist, weights)


def body(keys, cut, owner, tokens):
    tiles = tokens.reshape(EX // 8, 8, 16, 128).transpose(0, 2, 1, 3).reshape(EX * 16, 128)
    table, idx, src, tier, bins, hist, rows = exchange_stats(
        cut, keys.reshape(1, EX), owner.reshape(1, EX), tiles)
    branches = [functools.partial(exchange_rows, t) for t in range(len(TIERS))]
    rows, hist, weights, slots = lax.switch(tier[0], branches, cut, idx, src, rows, table, bins, hist)
    out, hist, weights = unpack_rows(slots.reshape(RECV), rows, hist, weights)
    packed_rows = out.reshape(RECV // 8, 16, 8, 128).transpose(0, 2, 1, 3).reshape(RECV, 16 * 128)
    return hist.reshape(BINS), packed_rows, weights.reshape(RECV)


def solution(mesh):
    torus = Mesh(mesh.devices.reshape(NY, NZ, NX, NC), AXES)
    return jax.shard_map(
        body,
        mesh=torus,
        in_specs=(P(AXES), P(), P(AXES, None), P(AXES, None)),
        out_specs=(P(), P(AXES, None), P(AXES)),
        check_vma=False,
    )
```

profile of v0, /device:TPU:1, one launch (start us, length us, event | category | flops | bytes accessed | tf_op | source)
XLA Modules:
  0.0 171.5 jit_solution(14879458493218820496)
XLA Ops:
  1.3 21.5 %exchange_stats.1 = (f32[32,8,1,128]{3,2,1,0:T(1,128)S(1)}, s32[8,128]{1,0:T(8,128)S(1)}, s32[7,128]{1,0:T(8,128)S(1)}, s32[1]{0:T(128)}, f32[8,1,128]{2,1,0:T(1...) custom-call(s32[1]{0:T(128)S(6)} %copy.23.cut_ref, s32[1,512]{1,0:T(1,128)} %bitcast.18, ...), custom_call_target="tpu_custom_call" | custom-call | tf_op jit(solution)/shard_map/exchange_stats/pallas_call | solution.py:264
  23.4 141.1 %conditional.1 = ((s32[1024,16,128]{2,1,0:T(8,128)S(1)}, s32[32,128]{1,0:T(8,128)S(1)}, f32[8,128]{1,0:T(8,128)S(1)}, s32[8,128]{1,0:T(8,128)S(1)})) conditional(s32[]{:T(128)} %bitcast.5, (s32[1]{0:T(128)}, s32[8,128]{1,0:T(8,128)S(1)}, s32[7,128]{1,0:T(8,128)S(1)}, s32[512,16,128]{2,1,0:T(8,128)S(1)}, ...), branch_computations={%region_0.0_spmd, %region_1.0_spmd, %region_2.0_spmd, %region_3.0_... | conditional | bytes 8 | solution.py:519
  23.6 140.6 %exchange_rows_1.1 = (s32[1024,16,128]{2,1,0:T(8,128)S(1)}, s32[32,128]{1,0:T(8,128)S(1)}, f32[8,128]{1,0:T(8,128)S(1)}, s32[8,128]{1,0:T(8,128)S(1)}) custom-call(s32[1]{0:T(128)} %get-tuple-element.85.cut_ref, s32[8,128]{1,0:T(8,128)S(1)} %get-tuple-element.86.idx_ref, s32[7,128]{1,0:T(8,128)S(1)} %get-tuple-element.87.src_ref, ...), custom_call_target="tpu_custom_call" | custom-call | tf_op jit(solution)/shard_map/cond/branch_1_fun/exchange_rows_1/pallas_call | solution.py:459
  164.5 7.0 %unpack_rows.1 = (s32[16384,128]{1,0:T(8,128)}, s32[32,128]{1,0:T(8,128)}, f32[8,128]{1,0:T(8,128)}) custom-call(s32[1024]{0:T(1024)S(1)} %bitcast.17, s32[1024,16,128]{2,1,0:T(8,128)S(1)} %get-tuple-element.158.rows_ref, s32[32,128]{1,0:T(8,128)S(1)} %get-tuple-element.157.hist_in, f32[8,128]{1,0:T(8,128)S(1)} %get-tuple-element.156.weight_in), custom_call_target="tpu_custom_call" | custom-call | tf_op jit(solution)/shard_map/unpack_rows/pallas_call | solution.py:503
where the time goes:
time: 172 us
  Pallas kernels  169 us (98%)
  between operations  1.91 us (1%)
    pallas_call x1, Pallas kernels, exchange_rows(): pl.pallas_call(functools.partial(main_kernel, caps), out_shape=(shape((NS...  141 us
    pallas_call x1, Pallas kernels, exchange_stats(): pl.pallas_call(stats_kernel, out_shape=(shape((PLANE, NZ, 1, 128), F32),...  21.5 us
    pallas_call x1, Pallas kernels, unpack_rows(): pl.pallas_call(unpack_kernel, grid=(RECV // block,), out_shape=(shape((RE...  6.99 us

commit v1 on v0

--- a/solution.py
+++ b/solution.py
@@ -21,13 +21,16 @@
 AXES = ("y", "z", "x", "c")
 
 TIERS = (
-    (204, 164, 118, 70),
-    (222, 180, 132, 84),
-    (254, 202, 154, 94),
+    (199, 161, 124, 104),
+    (210, 170, 141, 84),
+    (222, 179, 141, 90),
+    (245, 182, 141, 117),
+    (254, 200, 157, 101),
     (384, 264, 256, 128),
 )
 PLUS, OWN, MINUS = 0, 384, 512
 PACKED = 896
+HEAD = 40
 
 
 def me():
@@ -112,9 +115,9 @@
 
 
 def stats_kernel(cut_ref, keys_hbm, owner_hbm, tok_hbm,
-                 table_ref, idx_ref, src_ref, tier_ref, bins_ref, hist_ref, rows_ref,
-                 tok_ref, keys_ref, owner_ref, row_ref, ring_ref,
-                 tok_sem, keys_sem, owner_sem, send1, send2, recv1, recv2):
+                 table_ref, idx_ref, src_ref, tier_ref, bins_ref, hist_ref, rows_ref, up_ref, down_ref,
+                 tok_ref, keys_ref, owner_ref, row_ref, ring_ref, head_up, head_down, src_smem,
+                 tok_sem, keys_sem, owner_sem, src_sem, send1, send2, recv1, recv2, hsend, hrecv):
     y, z, x, c = me()
     load_keys = pltpu.make_async_copy(keys_hbm, keys_ref, keys_sem)
     load_owner = pltpu.make_async_copy(owner_hbm, owner_ref, owner_sem)
@@ -188,6 +191,26 @@
     for g in range(PACKED // 128):
         src_ref[pl.ds(g, 1), :] = jnp.sum(jnp.where(at == g * 128 + lane, e, 0), axis=0, keepdims=True)
 
+    src_ref[pl.ds(7, 1), :] = jnp.zeros((1, 128), I32)
+    copy = pltpu.make_async_copy(src_ref, src_smem, src_sem)
+    copy.start()
+
+    load.wait()
+
+    def tiled(b, k):
+        return tok_ref[pl.ds(b * 16 + (k // 8) * 128 + k % 8, 16, stride=8), :]
+
+    batched(0, EX, tiled, put(rows_ref))
+    copy.wait()
+    heads = []
+    for k, (start, buf, out, to) in enumerate((
+            (PLUS, head_up, up_ref, lax.rem(z + 1, NZ)), (MINUS, head_down, down_ref, lax.rem(z + NZ - 1, NZ)))):
+        batched(0, HEAD, lambda b, i, start=start: rows_ref[src_smem[start // 128, b + i]], put(buf), batch=8)
+        head = pltpu.make_async_remote_copy(
+            buf, out, hsend.at[k], hrecv.at[k], device_id={"z": to}, device_id_type=MESH_ID)
+        head.start()
+        heads.append(head)
+
     pltpu.make_async_copy(ring_ref.at[pl.ds(0, NZ - 1)], ring_ref.at[pl.ds(0, NZ - 1)], recv1).wait()
     p = y * NM + x * NC + c
 
@@ -211,26 +234,19 @@
     hist = mul(f32(iota((32, EX), 0) == bins >> 7), f32(iota((128, EX), 0) == bins & 127), (1, 1))
     hist_ref[...] = hist.reshape(32, 1, 128)
 
-    load.wait()
-
-    def tiled(b, k):
-        return tok_ref[pl.ds(b * 16 + (k // 8) * 128 + k % 8, 16, stride=8), :]
-
-    batched(0, EX, tiled, put(rows_ref))
-
     others = table_ref.at[pl.ds(0, PLANE - 1)]
     pltpu.make_async_copy(others, others, recv2).wait()
     every = table_ref[...].reshape(NS, 128)
 
     top = jnp.max(every, axis=0, keepdims=True)
     lane = iota((1, 128), 1)
-    tier = jnp.int32(0)
-    for caps in TIERS[:-1]:
+    tier = jnp.int32(len(TIERS) - 1)
+    for number, caps in reversed(list(enumerate(TIERS[:-1]))):
         cap = jnp.full((1, 128), 1e6, F32)
         for k in range(4):
             cap = jnp.where(lane == L_HOP + k, float(caps[k]), cap)
         over = jnp.where((lane >= L_HOP) & (lane < L_HOP + 4) & (top > cap), 1, 0)
-        tier = tier + jnp.max(over)
+        tier = jnp.where(jnp.max(over) == 0, number, tier)
     tier_ref[0] = tier
 
     zs, t = iota((NZ, NS), 0), iota((NZ, NS), 1)
@@ -254,6 +270,8 @@
 
     pltpu.make_async_copy(ring_ref.at[pl.ds(0, NZ - 1)], ring_ref.at[pl.ds(0, NZ - 1)], send1).wait()
     pltpu.make_async_copy(others, others, send2).wait()
+    for head in heads:
+        head.wait()
 
 
 def exchange_stats(cut, keys, owner, tokens):
@@ -266,21 +284,26 @@
         out_shape=(
             shape((PLANE, NZ, 1, 128), F32),
             shape((NZ, 128), I32),
-            shape((PACKED // 128, 128), I32),
+            shape((PACKED // 128 + 1, 128), I32),
             shape((1,), I32),
             shape((NZ, 1, 128), F32),
             shape((32, 1, 128), F32),
             shape((EX, 16, 128), I32),
+            shape((HEAD, 16, 128), I32),
+            shape((HEAD, 16, 128), I32),
         ),
         in_specs=[smem, hbm, hbm, hbm],
-        out_specs=(vmem, vmem, vmem, smem, vmem, vmem, vmem),
+        out_specs=(vmem, vmem, vmem, smem, vmem, vmem, vmem, vmem, vmem),
         scratch_shapes=[
             pltpu.VMEM((EX * 16, 128), I32),
             pltpu.VMEM((1, EX), I32),
             pltpu.VMEM((1, EX), I32),
             pltpu.VMEM((1, 1, 128), F32),
             pltpu.VMEM((NZ, 1, 128), F32),
-            *[dma] * 7,
+            pltpu.VMEM((HEAD, 16, 128), I32),
+            pltpu.VMEM((HEAD, 16, 128), I32),
+            pltpu.SMEM((PACKED // 128 + 1, 128), I32),
+            *[dma] * 8, dma((2,)), dma((2,)),
         ],
         compiler_params=pltpu.CompilerParams(
             collective_id=0, has_side_effects=True, vmem_limit_bytes=57 * 1024 * 1024),
@@ -288,7 +311,7 @@
     )(cut, keys, owner, tokens)
 
 
-def main_kernel(caps, cut_ref, idx_ref, src_ref, rows_ref, table_ref, bin_ref, hist_ref,
+def main_kernel(caps, cut_ref, idx_ref, src_ref, rows_ref, table_ref, bin_ref, hist_ref, up_ref, down_ref,
                 rows_out, hist_out, weight_out, slot_out,
                 pk, p1, m1, p2, m2, p3, m3, far, stage, hrs, hrow, hz, hrow2, hall, bz, ball,
                 zsend, zrecv, psend, precv, hs1, hr1, hs2, hr2, hs3, hr3, bs1, br1, bs2, br2):
@@ -324,14 +347,16 @@
     def pack(lo, hi):
         batched(lo, hi, lambda b, k: rows_ref[src_ref[(b + k) >> 7, (b + k) & 127]], put(pk))
 
-    pack(PLUS, PLUS + c1)
-    pack(MINUS, MINUS + c1)
+    pack(PLUS + HEAD, PLUS + c1)
+    pack(MINUS + HEAD, MINUS + c1)
     pl.semaphore_wait(bar, NZ - 1 + PLANE - 1)
 
     loop(1, NZ, lambda d: remote(bin_ref.at[lax.rem(z + d, NZ)], bz.at[z], bs1, br1, {"z": lax.rem(z + d, NZ)}))
-    h1 = [hop(pk, p1, 0, c2, PLUS, 0, 0, up), hop(pk, m1, 0, c2, MINUS, 0, 1, down),
+    h1 = [hop(pk, p1, HEAD, c2, PLUS, 0, 0, up), hop(pk, m1, HEAD, c2, MINUS, 0, 1, down),
           hop(pk, p1, c2, c1, PLUS, 0, 2, up), hop(pk, m1, c2, c1, MINUS, 0, 3, down)]
     bz[pl.ds(z, 1)] = bin_ref[pl.ds(z, 1)]
+    batched(0, HEAD, lambda b, k: up_ref[b + k], put(p1), batch=8)
+    batched(0, HEAD, lambda b, k: down_ref[b + k], put(m1), batch=8)
     pack(OWN, MINUS)
 
     def send_chunk(delta, src):
@@ -340,9 +365,13 @@
 
         batched(0, PLANE * 4, lambda b, k: src[idx_ref[zs, b + k]], lambda b, k, v: put(stage)(base + b, k, v))
         s = ((y * NZ + zs) * NX + x) * NC + c
-        loop(1, PLANE, lambda r: remote(
-            stage.at[pl.ds((delta * PLANE + r) * 4, 4)], rows_out.at[pl.ds(s * 4, 4)],
-            psend, precv, in_plane(r, y, x, c)))
+
+        def send(i):
+            r = lax.rem((c * (PLANE - i) + (1 - c) * i) * 13, PLANE)
+            remote(stage.at[pl.ds((delta * PLANE + r) * 4, 4)], rows_out.at[pl.ds(s * 4, 4)],
+                   psend, precv, in_plane(r, y, x, c))
+
+        loop(1, PLANE, send)
         pltpu.make_async_copy(
             stage.at[pl.ds(delta * PLANE * 4, 4)], rows_out.at[pl.ds(s * 4, 4)], precv).start()
 
@@ -448,7 +477,7 @@
     pltpu.make_async_copy(stage, rows_out, precv).wait()
 
 
-def exchange_rows(tier, cut, idx, src, rows, table, bins, hist):
+def exchange_rows(tier, cut, idx, src, rows, table, bins, hist, up, down):
     caps = TIERS[tier]
     c1, c2, c3, c4 = caps
     vmem, smem = pl.BlockSpec(memory_space=pltpu.VMEM), pl.BlockSpec(memory_space=pltpu.SMEM)
@@ -462,7 +491,7 @@
             shape((NS * 4, 16, 128), I32), shape((32, 128), I32),
             shape((RECV // 128, 128), F32), shape((RECV // 128, 128), I32),
         ),
-        in_specs=[smem, smem, smem, vmem, vmem, vmem, vmem],
+        in_specs=[smem, smem, smem, *[vmem] * 6],
         out_specs=(pl.BlockSpec(memory_space=pl.ANY), vmem, vmem, vmem),
         scratch_shapes=[
             rows_of(PACKED), rows_of(c1), rows_of(c1), rows_of(c2), rows_of(c2), rows_of(c3), rows_of(c3),
@@ -473,7 +502,7 @@
         compiler_params=pltpu.CompilerParams(
             collective_id=1 + tier, has_side_effects=True, vmem_limit_bytes=44 * 1024 * 1024),
         name=f"exchange_rows_{tier}",
-    )(cut, idx, src, rows, table, bins, hist)
+    )(cut, idx, src, rows, table, bins, hist, up, down)
 
 
 def unpack_kernel(slot_ref, rows_ref, hist_in, weight_in, out_ref, hist_out, weight_out):
@@ -513,10 +542,10 @@
 
 def body(keys, cut, owner, tokens):
     tiles = tokens.reshape(EX // 8, 8, 16, 128).transpose(0, 2, 1, 3).reshape(EX * 16, 128)
-    table, idx, src, tier, bins, hist, rows = exchange_stats(
+    table, idx, src, tier, bins, hist, rows, up, down = exchange_stats(
         cut, keys.reshape(1, EX), owner.reshape(1, EX), tiles)
     branches = [functools.partial(exchange_rows, t) for t in range(len(TIERS))]
-    rows, hist, weights, slots = lax.switch(tier[0], branches, cut, idx, src, rows, table, bins, hist)
+    rows, hist, weights, slots = lax.switch(tier[0], branches, cut, idx, src, rows, table, bins, hist, up, down)
     out, hist, weights = unpack_rows(slots.reshape(RECV), rows, hist, weights)
     packed_rows = out.reshape(RECV // 8, 16, 8, 128).transpose(0, 2, 1, 3).reshape(RECV, 16 * 128)
     return hist.reshape(BINS), packed_rows, weights.reshape(RECV)

time: 172 us -> 164 us (0.953); the launches traced: 172 us -> 166 us
  Pallas kernels: 169 us -> 164 us
    pallas_call x1, Pallas kernels: 141 us -> 133 us  [exchange_rows(): pl.pallas_call(functools.partial(main_kernel, caps), out_shape=(shape((NS...]
    pallas_call x1, Pallas kernels: 21.5 us -> 23.3 us  [exchange_stats(): pl.pallas_call(stats_kernel, out_shape=(shape((PLANE, NZ, 1, 128), F32),...]
where the time goes in v1:
time: 164 us; the launch traced here: 166 us
  Pallas kernels  164 us (100%)
  between operations  1.91 us (1%)
    pallas_call x1, Pallas kernels, exchange_rows(): pl.pallas_call(functools.partial(main_kernel, caps), out_shape=(shape((NS...  133 us
    pallas_call x1, Pallas kernels, exchange_stats(): pl.pallas_call(stats_kernel, out_shape=(shape((PLANE, NZ, 1, 128), F32),...  23.3 us
    pallas_call x1, Pallas kernels, unpack_rows(): pl.pallas_call(unpack_kernel, grid=(RECV // block,), out_shape=(shape((RE...  6.99 us

profile of v1, /device:TPU:1, one launch (start us, length us, event | category | flops | bytes accessed | tf_op | source)
XLA Modules:
  0.0 166.2 jit_solution(5208965194892432261)
XLA Ops:
  1.3 23.3 %exchange_stats.1 = (f32[32,8,1,128]{3,2,1,0:T(1,128)S(1)}, s32[8,128]{1,0:T(8,128)S(1)}, s32[8,128]{1,0:T(8,128)S(1)}, s32[1]{0:T(128)}, f32[8,1,128]{2,1,0:T(1...) custom-call(s32[1]{0:T(128)S(6)} %copy.31.cut_ref, ...), custom_call_target="tpu_custom_call" | custom-call | tf_op jit(solution)/shard_map/exchange_stats/pallas_call | solution.py:282
  25.2 134.0 %conditional.1 = ((s32[1024,16,128]{2,1,0:T(8,128)S(1)}, s32[32,128]{1,0:T(8,128)S(1)}, f32[8,128]{1,0:T(8,128)S(1)}, s32[8,128]{1,0:T(8,128)S(1)})) conditional(s32[]{:T(128)} %bitcast.5, (s32[1]{0:T(128)}, s32[8,128]{1,0:T(8,128)S(1)}, s32[8,128]{1,0:T(8,128)S(1)}, s32[512,16,128]{2,1,0:T(8,128)S(1)}, ...), branch_computations={%region_0.0_spmd, %region_1.0_spmd, %region_2.0_spmd, %region_3.0_... | conditional | bytes 8 | solution.py:548
  25.5 133.2 %exchange_rows_2.1 = (s32[1024,16,128]{2,1,0:T(8,128)S(1)}, s32[32,128]{1,0:T(8,128)S(1)}, f32[8,128]{1,0:T(8,128)S(1)}, s32[8,128]{1,0:T(8,128)S(1)}) custom-call(s32[1]{0:T(128)} %get-tuple-element.156.cut_ref, s32[8,128]{1,0:T(8,128)S(1)} %get-tuple-element.157.idx_ref, s32[8,128]{1,0:T(8,128)S(1)} %get-tuple-element.158.src_ref, ...), custom_call_target="tpu_custom_call" | custom-call | tf_op jit(solution)/shard_map/cond/branch_2_fun/exchange_rows_2/pallas_call | solution.py:488
  159.2 7.0 %unpack_rows.1 = (s32[16384,128]{1,0:T(8,128)}, s32[32,128]{1,0:T(8,128)}, f32[8,128]{1,0:T(8,128)}) custom-call(s32[1024]{0:T(1024)S(1)} %bitcast.17, s32[1024,16,128]{2,1,0:T(8,128)S(1)} %get-tuple-element.256.rows_ref, s32[32,128]{1,0:T(8,128)S(1)} %get-tuple-element.255.hist_in, f32[8,128]{1,0:T(8,128)S(1)} %get-tuple-element.254.weight_in), custom_call_target="tpu_custom_call" | custom-call | tf_op jit(solution)/shard_map/unpack_rows/pallas_call | solution.py:532
